TPU v7x, 32 devices: a whole 2x2x4 slice. The times are simulated.
32 devices in a mesh: gx: 4 (over y, core), gy: 8 (over z, x).
Axes of the slice: x: 2, y: 2, z: 4, core: 2. Of those that a mesh axis runs over, the one named last changes fastest.
Arguments:
- spectra: bfloat16 [4, 8, 3, 2, 128, 4096], P('gx', 'gy'), may hold values from -1000 to 1000
- partner_codes: int32 [4, 8, 5], P('gx', 'gy'), may hold values from -1 to 4, as said below
- range_bits: int32 [4, 8, 5, 128, 5], P('gx', 'gy'), may hold values from 0 to 1073741823
- old_stacks: float32 [4, 8, 5, 8, 2, 128, 128], P('gx', 'gy'), may hold values from -6 to 6
Outputs:
- stacks: float32 [4, 8, 5, 8, 2, 128, 128], P('gx', 'gy')
Inputs may be any that keep to these rules, and one draw needn't show every extreme that they name: `partner_codes`: each block lists code 0 first, then further distinct codes in increasing order, then -1 in the remaining slots; no listed code names a block outside the grid of 4 x 8 blocks; some block lists all 5 codes.
All inputs are finite; a program needn't handle non-finite values.
Results may differ from a plain program's by a relative error of at most 0.0014.
Values may be sent and summed in bfloat16 or wider, within the bound.
A program may use at most 192 MiB of HBM per device.

v0:
```python
import functools
import math

import jax
import jax.numpy as jnp
from jax import lax
from jax.experimental import pallas as pl
from jax.experimental.pallas import tpu as pltpu
from jax.sharding import PartitionSpec as P

EPSILON = 1e-06
MESH = pl.DeviceIdType.MESH
FLAG_BITS = 30


def whiten_block(ref, index):
    segments, parts, stations, width = ref.shape[len(index):]
    chunk = 16

    def rows(i, _):
        at = pl.ds(pl.multiple_of(i * chunk, chunk), chunk)
        pieces = [ref[(*index, s, p, at)].astype(jnp.float32)
                  for s in range(segments) for p in range(parts)]
        total = pieces[0] * pieces[0]
        for v in pieces[1:]:
            total = total + v * v
        power = jnp.sum(total, axis=1, keepdims=True) * (1.0 / (len(pieces) * width))
        scale = lax.rsqrt(power + EPSILON)
        for s in range(segments):
            for p in range(parts):
                ref[(*index, s, p, at)] = (pieces[s * parts + p] * scale).astype(jnp.bfloat16)
        return 0

    lax.fori_loop(0, stations // chunk, rows, 0, unroll=2)


def product(left, right, scale):
    segments = left.count
    total = None
    for s in range(segments):
        part = lax.dot_general(
            left(s), right(s), (((1,), (1,)), ((), ())), preferred_element_type=jnp.float32
        )
        total = part if total is None else total + part
    n = total.shape[0] // 2
    real = total[:n, :n] + total[n:, n:]
    imag = total[n:, :n] - total[:n, n:]
    return real * scale, imag * scale


class View:
    def __init__(self, ref, index, count):
        self.ref, self.index, self.count = ref, index, count

    def __call__(self, s):
        v = self.ref[(*self.index, s)]
        return v.reshape(v.shape[0] * v.shape[1], v.shape[2])


OTHER = 3


def cross_kernel(rows, cols, x_ref, self_ref, c_ref, blk, stage,
                 load_sem, xs, xr, zs, zr, ys, yr, rs, rr):
    half, segments, width = blk.shape[1], blk.shape[3], blk.shape[6]
    scale = 1.0 / math.sqrt(segments * width)
    r = lax.axis_index("gx")
    c = lax.axis_index("gy")
    odd = lax.rem(c, 2)
    mate = c + 1 - 2 * odd
    keep_slot = 2 * odd
    halo_slot = 2 - 2 * odd
    z_to = c - 2 + 4 * odd
    z_from = c + 2 - 4 * odd
    sends_z = (z_to >= 0) & (z_to < cols)
    has_halo = (z_from >= 0) & (z_from < cols)
    first_col = c - 2 * odd

    def load(b, mine):
        band = half * (odd if mine else 1 - odd) + b
        at = pl.ds(pl.multiple_of(band * width, width), width)
        slot = keep_slot if mine else OTHER
        return pltpu.make_async_copy(
            x_ref.at[0, 0, :, :, :, at], blk.at[0, b, slot], load_sem.at[int(mine), b])

    def x_copy(b, s):
        return pltpu.make_async_remote_copy(
            src_ref=blk.at[0, b, OTHER, s], dst_ref=blk.at[0, b, 1, s],
            send_sem=xs.at[b, s], recv_sem=xr.at[b, s],
            device_id=(r, mate), device_id_type=MESH)

    def z_copy(b, s):
        return pltpu.make_async_remote_copy(
            src_ref=blk.at[0, b, keep_slot, s], dst_ref=blk.at[0, b, halo_slot, s],
            send_sem=zs.at[b, s], recv_sem=zr.at[b, s], device_id=(r, z_to), device_id_type=MESH)

    def y_row(b):
        return r - 1 + 2 * lax.rem(b, 2)

    def y_sends(b):
        to = y_row(b)
        return (to >= 0) & (to < rows)

    def y_meets(b):
        other_row = r + 1 - 2 * lax.rem(b, 2)
        return (other_row >= 0) & (other_row < rows)

    def y_copy(b, slot, s):
        return pltpu.make_async_remote_copy(
            src_ref=blk.at[0, b, slot, s], dst_ref=blk.at[1, b, slot, s],
            send_sem=ys.at[b, slot, s], recv_sem=yr.at[b, slot, s],
            device_id=(y_row(b), c), device_id_type=MESH)

    def r_copy(b, which, code, band, row, col):
        return pltpu.make_async_remote_copy(
            src_ref=stage.at[b, which], dst_ref=c_ref.at[code - 1, band],
            send_sem=rs.at[b, which], recv_sem=rr.at[code - 1, band],
            device_id=(row, col), device_id_type=MESH)

    def load_band(b, _):
        pl.when(b > 0)(load(b, False).start)
        load(b, True).start()
        return 0

    def send_band(b, _):
        @pl.when(b > 0)
        def _():
            load(b, False).wait()
            whiten_block(blk, (0, b, OTHER))

        for s in range(segments):
            x_copy(b, s).start()
        load(b, True).wait()
        whiten_block(blk, (0, b, keep_slot))

        @pl.when(sends_z)
        def _():
            for s in range(segments):
                z_copy(b, s).start()

        @pl.when(y_sends(b))
        def _():
            for slot in (keep_slot, OTHER):
                for s in range(segments):
                    y_copy(b, slot, s).start()
        return 0

    load(0, False).start()
    barrier = pltpu.get_barrier_semaphore()
    peers = jnp.int32(0)
    for dr in (-1, 0, 1):
        for col in (mate, c - 2, c + 2) if dr == 0 else (c, mate, c - 2, c + 2):
            there = (r + dr >= 0) & (r + dr < rows) & (col >= 0) & (col < cols)
            peers = peers + there.astype(jnp.int32)

            @pl.when(there)
            def _():
                pl.semaphore_signal(barrier, inc=1, device_id=(r + dr, col), device_id_type=MESH)
    load(0, False).wait()
    lax.fori_loop(0, half, load_band, 0)
    whiten_block(blk, (0, 0, OTHER))
    pl.semaphore_wait(barrier, peers)
    lax.fori_loop(0, half, send_band, 0)

    def own_product(b, _):
        for slot, band in ((keep_slot, half * odd + b), (OTHER, half * (1 - odd) + b)):
            view = View(blk, (0, b, slot), segments)
            real, imag = product(view, view, scale)
            self_ref[band, 0] = real
            self_ref[band, 1] = imag
        return 0

    left_pair = (odd == 0) | has_halo
    right_pair = (odd == 1) | has_halo

    def routes(b):
        is_odd = lax.rem(b, 2)
        meets = y_meets(b)
        top = r - is_odd
        t, m = is_odd, 1 - is_odd
        band, other_band = half * odd + b, half * (1 - odd) + b
        return [
            (0, (0, 0), (0, 1), 3, band, r, first_col, left_pair, odd == 0),
            (1, (0, 1), (0, 2), 3, band, r, mate, right_pair, None),
            (2, (t, keep_slot), (m, keep_slot), 1, band, top, c, meets, is_odd == 0),
            (3, (t, OTHER), (m, OTHER), 1, other_band, top, c, meets, is_odd == 0),
            (4, (t, 0), (m, 1), 4, band, top, first_col, meets & left_pair, (odd == 0) & (is_odd == 0)),
            (5, (t, 1), (m, 2), 4, band, top, mate, meets & right_pair, None),
            (6, (m, 0), (t, 1), 2, band, top + 1, first_col, meets & left_pair, (odd == 0) & (is_odd == 1)),
            (7, (m, 1), (t, 2), 2, band, top + 1, mate, meets & right_pair, None),
        ]

    def emit(b, route, go=True):
        which, left, right, code, band, row, col, present, local = route

        @pl.when(present)
        def _():
            real, imag = product(View(blk, (left[0], b, left[1]), segments),
                                 View(blk, (right[0], b, right[1]), segments), scale)
            real, imag = real.astype(jnp.bfloat16), imag.astype(jnp.bfloat16)

            def remote():
                stage[b, which, 0] = real
                stage[b, which, 1] = imag
                pl.when(go)(r_copy(b, which, code, band, row, col).start)

            if local is None:
                remote()
            else:
                @pl.when(local)
                def _():
                    c_ref[code - 1, band, 0] = real
                    c_ref[code - 1, band, 1] = imag

                pl.when(jnp.logical_not(local))(remote)

    def step(b, _):
        @pl.when(b < half)
        def _():
            for s in range(segments):
                x_copy(b, s).wait_recv()

                @pl.when(y_sends(b))
                def _():
                    y_copy(b, 1, s).start()

                @pl.when(has_halo)
                def _():
                    z_copy(b, s).wait_recv()

                    @pl.when(y_sends(b))
                    def _():
                        y_copy(b, halo_slot, s).start()

            @pl.when(b == half - 1)
            def _():
                for a in range(half - 1):
                    table = routes(a)
                    for which in (1, 5, 7) if a < half - 2 else (1,):
                        _, _, _, code, band, row, col, present, _ = table[which]
                        pl.when(present)(r_copy(a, which, code, band, row, col).start)

            @pl.when(y_meets(b))
            def _():
                for slot in (keep_slot, OTHER):
                    for s in range(segments):
                        y_copy(b, slot, s).wait_recv()

            table = routes(b)
            for which in (1, 0, 2, 3):
                emit(b, table[which], b == half - 1 if which == 1 else True)

        @pl.when(b > 0)
        def _():
            a = b - 1

            @pl.when(y_meets(a))
            def _():
                for s in range(segments):
                    y_copy(a, 1, s).wait_recv()

                @pl.when(has_halo)
                def _():
                    for s in range(segments):
                        y_copy(a, halo_slot, s).wait_recv()

            table = routes(a)
            for which in (5, 7, 4, 6):
                emit(a, table[which], a >= half - 2 if which in (5, 7) else True)
        return 0

    lax.fori_loop(0, half, own_product, 0)
    lax.fori_loop(0, half + 1, step, 0)

    def finish(b, _):
        for s in range(segments):
            x_copy(b, s).wait_send()

            @pl.when(sends_z)
            def _():
                z_copy(b, s).wait_send()

            @pl.when(y_sends(b))
            def _():
                for slot in (keep_slot, OTHER, 1):
                    y_copy(b, slot, s).wait_send()

                @pl.when(has_halo)
                def _():
                    y_copy(b, halo_slot, s).wait_send()

        for which, _, _, code, band, row, col, present, local in routes(b):
            gone = present if local is None else present & jnp.logical_not(local)

            @pl.when(gone)
            def _():
                r_copy(b, which, code, band, row, col).wait_send()
        return 0

    lax.fori_loop(0, half, finish, 0)

    next_col = c + 1 < cols
    below = r + 1 < rows
    above = r > 0

    def arrive(g, _):
        part = g // half
        b = g - part * half
        is_odd = lax.rem(b, 2)
        here = (odd == 0) & (part == 0)
        arrivals = [
            (1, below & (is_odd == 1)),
            (2, above & next_col & jnp.logical_not(here & (is_odd == 1))),
            (3, next_col & jnp.logical_not(here)),
            (4, below & next_col & jnp.logical_not(here & (is_odd == 0))),
        ]
        for code, remote in arrivals:
            @pl.when(remote)
            def _():
                pltpu.make_async_remote_copy(
                    src_ref=stage.at[0, 0], dst_ref=c_ref.at[code - 1, g],
                    send_sem=rs.at[0, 0], recv_sem=rr.at[code - 1, g],
                    device_id=(r, mate), device_id_type=MESH).wait_recv()
        return 0

    lax.fori_loop(0, 2 * half, arrive, 0)


def crosses(spectra, bands, rows, cols):
    segments, parts, stations, bins = spectra.shape[2:]
    half, width = bands // 2, bins // bands
    dma = pltpu.SemaphoreType.DMA
    return pl.pallas_call(
        functools.partial(cross_kernel, rows, cols),
        out_shape=(
            jax.ShapeDtypeStruct((bands, 2, stations, stations), jnp.float32),
            jax.ShapeDtypeStruct((4, bands, 2, stations, stations), jnp.bfloat16),
        ),
        in_specs=[pl.BlockSpec(memory_space=pltpu.MemorySpace.HBM)],
        out_specs=(pl.BlockSpec(memory_space=pltpu.VMEM), pl.BlockSpec(memory_space=pltpu.VMEM)),
        scratch_shapes=[
            pltpu.VMEM((2, half, 4, segments, parts, stations, width), jnp.bfloat16),
            pltpu.VMEM((half, 8, 2, stations, stations), jnp.bfloat16),
            dma((2, half)),
            dma((half, segments)), dma((half, segments)),
            dma((half, segments)), dma((half, segments)),
            dma((half, 4, segments)), dma((half, 4, segments)),
            dma((half, 8)), dma((4, bands)),
        ],
        compiler_params=pltpu.CompilerParams(collective_id=0, has_side_effects=True, vmem_limit_bytes=48 * 1024 * 1024),
        name="crosses",
    )(spectra)


def combine_kernel(codes, self_ref, c_ref, bits_ref, old_ref, out_ref, done, sem):
    slots, bands = old_ref.shape[2:4]
    words, stations = bits_ref.shape[2], bits_ref.shape[4]
    column = lax.broadcasted_iota(jnp.int32, (stations, stations), 0)

    def write(s):
        return pltpu.make_async_copy(done.at[s], out_ref.at[0, 0, s], sem.at[s])

    for s in range(slots):
        code = codes[s]
        chosen = jnp.zeros((stations, stations), jnp.int32)
        bit = column
        for w in range(words):
            reached = column >= w * FLAG_BITS
            chosen = jnp.where(reached, bits_ref[0, s, w], chosen)
            bit = jnp.where(reached, column - w * FLAG_BITS, bit)
        flags = jnp.bitwise_and(jnp.right_shift(chosen, bit), 1).astype(jnp.float32).T > 0.5

        @pl.when(code == 0)
        def _():
            for k in range(bands):
                done[s, k] = old_ref[0, 0, s, k] + jnp.where(flags, self_ref[k], 0.0)

        @pl.when(code > 0)
        def _():
            for k in range(bands):
                done[s, k] = old_ref[0, 0, s, k] + jnp.where(
                    flags, c_ref[code - 1, k].astype(jnp.float32), 0.0)

        @pl.when(code < 0)
        def _():
            done[s] = old_ref[0, 0, s]

        write(s).start()
    for s in range(slots):
        write(s).wait()


def combine(codes, own, cross, range_bits, old):
    slots, bands, parts, stations = old.shape[2:6]
    vmem = pl.BlockSpec(memory_space=pltpu.VMEM)
    return pl.pallas_call(
        combine_kernel,
        out_shape=jax.ShapeDtypeStruct(old.shape, old.dtype),
        in_specs=[pl.BlockSpec(memory_space=pltpu.SMEM), vmem, vmem, vmem, vmem],
        out_specs=pl.BlockSpec(memory_space=pltpu.MemorySpace.HBM),
        scratch_shapes=[
            pltpu.VMEM((slots, bands, parts, stations, stations), jnp.float32),
            pltpu.SemaphoreType.DMA((slots,)),
        ],
        compiler_params=pltpu.CompilerParams(vmem_limit_bytes=20 * 1024 * 1024),
        name="combine",
    )(codes, own, cross, jnp.transpose(range_bits, (0, 2, 4, 1, 3)), old)


def solution(mesh):
    rows, cols = mesh.shape["gx"], mesh.shape["gy"]

    def body(spectra, partner_codes, range_bits, old_stacks):
        own, cross = crosses(spectra, old_stacks.shape[3], rows, cols)
        return combine(partner_codes[0, 0], own, cross, range_bits, old_stacks)

    return jax.shard_map(
        body,
        mesh=mesh,
        in_specs=(
            P("gx", "gy", None, None, None, None),
            P("gx", "gy", None),
            P("gx", "gy", None, None, None),
            P("gx", "gy", None, None, None, None, None),
        ),
        out_specs=P("gx", "gy", None, None, None, None, None),
        check_vma=False,
    )
```

profile of v0, /device:TPU:11, one launch (start us, length us, event | category | flops | bytes accessed | tf_op | source)
XLA Modules:
  0.0 95.7 jit_solution(8242111378067275510)
XLA Ops:
  0.0 0.0 copy-start
  0.0 0.0 copy-start.1
  0.0 0.0 copy-start.2
  0.0 92.5 %crosses.1 = (f32[8,2,128,128]{3,2,1,0:T(8,128)S(1)}, bf16[4,8,2,128,128]{4,3,2,1,0:T(8,128)(2,1)S(1)}) custom-call(bf16[1,1,3,2,128,4096]{5,4,3,2,1,0:T(8,128)(2,1)} %x_ref.1), custom_call_target="tpu_custom_call" | custom-call | tf_op jit(solution)/shard_map/crosses/pallas_call | solution.py:333
  92.5 0.0 copy-done
  92.6 0.0 copy-done.1
  92.6 0.0 copy-done.2
  92.6 3.1 %combine.1 = f32[1,1,5,8,2,128,128]{6,5,4,3,2,1,0:T(8,128)} custom-call(s32[5]{0:T(128)S(1)} %bitcast.3, f32[8,2,128,128]{3,2,1,0:T(8,128)S(1)} %get-tuple-element.7.self_ref, bf16[4,8,2,128,128]{4,3,2,1,0:T(8,128)(2,1)S(1)} %get-tuple-element.8.c_ref, s32[1,5,5,1,128]{4,3,2,1,0:T(1,128)S(1)} %bitcast.2, f32[1,1,5,8,2,128,128]{6,5,4,3,2,1,0:T(8,128)S(1)} %copy-done), custom_call_target="tpu_custom_call" | custom-call | tf_op jit(solution)/shard_map/combine/pallas_call | solution.py:396
Async XLA Ops:
  0.0 92.5 %copy-start = (f32[1,1,5,8,2,128,128]{6,5,4,3,2,1,0:T(8,128)S(1)}, f32[1,1,5,8,2,128,128]{6,5,4,3,2,1,0:T(8,128)}, u32[]{:S(2)}) copy-start(f32[1,1,5,8,2,128,128]{6,5,4,3,2,1,0:T(8,128)} %old_ref.1) | copy-start | bytes 15728644
  0.0 92.6 %copy-start.1 = (s32[1,1,5,128,5]{3,1,4,2,0:T(1,128)S(1)}, s32[1,1,5,128,5]{3,1,4,2,0:T(1,128)}, u32[]{:S(2)}) copy-start(s32[1,1,5,128,5]{3,1,4,2,0:T(1,128)} %param.6) | copy-start | bytes 38404
  0.0 92.6 %copy-start.2 = (s32[1,1,5]{2,1,0:T(1,128)S(1)}, s32[1,1,5]{2,1,0:T(1,128)}, u32[]{:S(2)}) copy-start(s32[1,1,5]{2,1,0:T(1,128)} %param.5) | copy-start | bytes 64
where the time goes:
time: 95.9 us; the launch traced here: 95.7 us
  Pallas kernels  95.7 us (100%)
    pallas_call x1, Pallas kernels, crosses(): pl.pallas_call(functools.partial(cross_kernel, rows, cols), out_shape=(ja...  92.5 us
    pallas_call x1, Pallas kernels, combine(): pl.pallas_call(combine_kernel, out_shape=jax.ShapeDtypeStruct(old.shape,...  3.14 us

commit v1 on v0

--- a/solution.py
+++ b/solution.py
@@ -86,13 +86,13 @@
     def x_copy(b, s):
         return pltpu.make_async_remote_copy(
             src_ref=blk.at[0, b, OTHER, s], dst_ref=blk.at[0, b, 1, s],
-            send_sem=xs.at[b, s], recv_sem=xr.at[b, s],
+            send_sem=xs.at[0], recv_sem=xr.at[b, s],
             device_id=(r, mate), device_id_type=MESH)
 
     def z_copy(b, s):
         return pltpu.make_async_remote_copy(
             src_ref=blk.at[0, b, keep_slot, s], dst_ref=blk.at[0, b, halo_slot, s],
-            send_sem=zs.at[b, s], recv_sem=zr.at[b, s], device_id=(r, z_to), device_id_type=MESH)
+            send_sem=zs.at[0], recv_sem=zr.at[b, s], device_id=(r, z_to), device_id_type=MESH)
 
     def y_row(b):
         return r - 1 + 2 * lax.rem(b, 2)
@@ -105,17 +105,30 @@
         other_row = r + 1 - 2 * lax.rem(b, 2)
         return (other_row >= 0) & (other_row < rows)
 
-    def y_copy(b, slot, s):
+    def y_copy(b, slot, s, group=0):
         return pltpu.make_async_remote_copy(
             src_ref=blk.at[0, b, slot, s], dst_ref=blk.at[1, b, slot, s],
-            send_sem=ys.at[b, slot, s], recv_sem=yr.at[b, slot, s],
+            send_sem=ys.at[b], recv_sem=yr.at[b, group],
             device_id=(y_row(b), c), device_id_type=MESH)
 
+    def y_taken(b, slots, group):
+        return pltpu.make_async_remote_copy(
+            src_ref=blk.at[0, b, pl.ds(0, slots)], dst_ref=blk.at[1, b, pl.ds(0, slots)],
+            send_sem=ys.at[b], recv_sem=yr.at[b, group],
+            device_id=(y_row(b), c), device_id_type=MESH)
+
     def r_copy(b, which, code, band, row, col):
+        group = {1: 0, 0: 1, 2: 2, 3: 2, 5: 3, 7: 3, 4: 5, 6: 7}[which]
         return pltpu.make_async_remote_copy(
             src_ref=stage.at[b, which], dst_ref=c_ref.at[code - 1, band],
-            send_sem=rs.at[b, which], recv_sem=rr.at[code - 1, band],
+            send_sem=rs.at[group + lax.rem(b, 2) if group > 2 else group], recv_sem=rr.at[code - 1],
             device_id=(row, col), device_id_type=MESH)
+
+    def r_whole(group, code, count):
+        return pltpu.make_async_remote_copy(
+            src_ref=c_ref.at[0, pl.ds(0, count)], dst_ref=c_ref.at[0, pl.ds(0, count)],
+            send_sem=rs.at[group], recv_sem=rr.at[code - 1],
+            device_id=(r, mate), device_id_type=MESH)
 
     def load_band(b, _):
         pl.when(b > 0)(load(b, False).start)
@@ -222,7 +235,7 @@
 
                 @pl.when(y_sends(b))
                 def _():
-                    y_copy(b, 1, s).start()
+                    y_copy(b, 1, s, 1).start()
 
                 @pl.when(has_halo)
                 def _():
@@ -230,7 +243,7 @@
 
                     @pl.when(y_sends(b))
                     def _():
-                        y_copy(b, halo_slot, s).start()
+                        y_copy(b, halo_slot, s, 2).start()
 
             @pl.when(b == half - 1)
             def _():
@@ -242,9 +255,7 @@
 
             @pl.when(y_meets(b))
             def _():
-                for slot in (keep_slot, OTHER):
-                    for s in range(segments):
-                        y_copy(b, slot, s).wait_recv()
+                y_taken(b, 2, 0).wait_recv()
 
             table = routes(b)
             for which in (1, 0, 2, 3):
@@ -256,13 +267,11 @@
 
             @pl.when(y_meets(a))
             def _():
-                for s in range(segments):
-                    y_copy(a, 1, s).wait_recv()
+                y_taken(a, 1, 1).wait_recv()
 
                 @pl.when(has_halo)
                 def _():
-                    for s in range(segments):
-                        y_copy(a, halo_slot, s).wait_recv()
+                    y_taken(a, 1, 2).wait_recv()
 
             table = routes(a)
             for which in (5, 7, 4, 6):
@@ -272,58 +281,48 @@
     lax.fori_loop(0, half, own_product, 0)
     lax.fori_loop(0, half + 1, step, 0)
 
+    def sent(slots, index, sem):
+        return pltpu.make_async_remote_copy(
+            src_ref=slots, dst_ref=slots, send_sem=sem.at[index], recv_sem=xr.at[0, 0],
+            device_id=(r, mate), device_id_type=MESH)
+
+    sent(blk.at[0, :, OTHER], 0, xs).wait_send()
+
+    @pl.when(sends_z)
+    def _():
+        sent(blk.at[0, :, OTHER], 0, zs).wait_send()
+
     def finish(b, _):
-        for s in range(segments):
-            x_copy(b, s).wait_send()
-
-            @pl.when(sends_z)
-            def _():
-                z_copy(b, s).wait_send()
-
-            @pl.when(y_sends(b))
-            def _():
-                for slot in (keep_slot, OTHER, 1):
-                    y_copy(b, slot, s).wait_send()
-
-                @pl.when(has_halo)
-                def _():
-                    y_copy(b, halo_slot, s).wait_send()
-
-        for which, _, _, code, band, row, col, present, local in routes(b):
-            gone = present if local is None else present & jnp.logical_not(local)
-
-            @pl.when(gone)
-            def _():
-                r_copy(b, which, code, band, row, col).wait_send()
+        @pl.when(y_sends(b) & has_halo)
+        def _():
+            sent(blk.at[0, b], b, ys).wait_send()
+
+        @pl.when(y_sends(b) & jnp.logical_not(has_halo))
+        def _():
+            sent(blk.at[0, b, pl.ds(0, 3)], b, ys).wait_send()
         return 0
 
     lax.fori_loop(0, half, finish, 0)
+
+    turns = [(half + 1 - parity) // 2 for parity in (0, 1)]
+    pl.when(right_pair)(r_whole(0, 1, half).wait_send)
+    pl.when(left_pair & (odd == 1))(r_whole(1, 1, half).wait_send)
+    pl.when(y_meets(1))(r_whole(2, 1, 2 * turns[1]).wait_send)
+    for parity in (0, 1):
+        meets = y_meets(parity)
+        pl.when(meets & right_pair)(r_whole(3 + parity, 1, 2 * turns[parity]).wait_send)
+        for group, near in ((5, parity == 0), (7, parity == 1)):
+            gone = meets & left_pair & ((odd == 1) if near else True)
+            pl.when(gone)(r_whole(group + parity, 1, turns[parity]).wait_send)
 
     next_col = c + 1 < cols
     below = r + 1 < rows
     above = r > 0
-
-    def arrive(g, _):
-        part = g // half
-        b = g - part * half
-        is_odd = lax.rem(b, 2)
-        here = (odd == 0) & (part == 0)
-        arrivals = [
-            (1, below & (is_odd == 1)),
-            (2, above & next_col & jnp.logical_not(here & (is_odd == 1))),
-            (3, next_col & jnp.logical_not(here)),
-            (4, below & next_col & jnp.logical_not(here & (is_odd == 0))),
-        ]
-        for code, remote in arrivals:
-            @pl.when(remote)
-            def _():
-                pltpu.make_async_remote_copy(
-                    src_ref=stage.at[0, 0], dst_ref=c_ref.at[code - 1, g],
-                    send_sem=rs.at[0, 0], recv_sem=rr.at[code - 1, g],
-                    device_id=(r, mate), device_id_type=MESH).wait_recv()
-        return 0
-
-    lax.fori_loop(0, 2 * half, arrive, 0)
+    pl.when(below)(r_whole(0, 1, 2 * turns[1]).wait_recv)
+    for code, comes, near in ((2, above & next_col, turns[1]), (3, next_col, half),
+                              (4, below & next_col, turns[0])):
+        pl.when(comes & (odd == 1))(r_whole(0, code, 2 * half).wait_recv)
+        pl.when(comes & (odd == 0))(r_whole(0, code, 2 * half - near).wait_recv)
 
 
 def crosses(spectra, bands, rows, cols):
@@ -342,10 +341,10 @@
             pltpu.VMEM((2, half, 4, segments, parts, stations, width), jnp.bfloat16),
             pltpu.VMEM((half, 8, 2, stations, stations), jnp.bfloat16),
             dma((2, half)),
-            dma((half, segments)), dma((half, segments)),
-            dma((half, segments)), dma((half, segments)),
-            dma((half, 4, segments)), dma((half, 4, segments)),
-            dma((half, 8)), dma((4, bands)),
+            dma((1,)), dma((half, segments)),
+            dma((1,)), dma((half, segments)),
+            dma((half,)), dma((half, 3)),
+            dma((9,)), dma((4,)),
         ],
         compiler_params=pltpu.CompilerParams(collective_id=0, has_side_effects=True, vmem_limit_bytes=48 * 1024 * 1024),
         name="crosses",

time: 95.9 us -> 94.5 us (0.985)
  Pallas kernels: 95.7 us -> 94.3 us
    pallas_call x1, Pallas kernels: 92.5 us -> 91.1 us  [crosses(): pl.pallas_call(functools.partial(cross_kernel, rows, cols), out_shape=(ja...]
where the time goes in v1:
time: 94.5 us; the launch traced here: 94.3 us
  Pallas kernels  94.3 us (100%)
    pallas_call x1, Pallas kernels, crosses(): pl.pallas_call(functools.partial(cross_kernel, rows, cols), out_shape=(ja...  91.1 us
    pallas_call x1, Pallas kernels, combine(): pl.pallas_call(combine_kernel, out_shape=jax.ShapeDtypeStruct(old.shape,...  3.14 us

profile of v1, /device:TPU:11, one launch (start us, length us, event | category | flops | bytes accessed | tf_op | source)
XLA Modules:
  0.0 94.3 jit_solution(12876068875129351469)
XLA Ops:
  0.0 0.0 copy-start
  0.0 0.0 copy-start.1
  0.0 0.0 copy-start.2
  0.0 91.1 %crosses.1 = (f32[8,2,128,128]{3,2,1,0:T(8,128)S(1)}, bf16[4,8,2,128,128]{4,3,2,1,0:T(8,128)(2,1)S(1)}) custom-call(bf16[1,1,3,2,128,4096]{5,4,3,2,1,0:T(8,128)(2,1)} %x_ref.1), custom_call_target="tpu_custom_call" | custom-call | tf_op jit(solution)/shard_map/crosses/pallas_call | solution.py:332
  91.1 0.0 copy-done
  91.2 0.0 copy-done.1
  91.2 0.0 copy-done.2
  91.2 3.1 %combine.1 = f32[1,1,5,8,2,128,128]{6,5,4,3,2,1,0:T(8,128)} custom-call(s32[5]{0:T(128)S(1)} %bitcast.3, f32[8,2,128,128]{3,2,1,0:T(8,128)S(1)} %get-tuple-element.7.self_ref, bf16[4,8,2,128,128]{4,3,2,1,0:T(8,128)(2,1)S(1)} %get-tuple-element.8.c_ref, s32[1,5,5,1,128]{4,3,2,1,0:T(1,128)S(1)} %bitcast.2, f32[1,1,5,8,2,128,128]{6,5,4,3,2,1,0:T(8,128)S(1)} %copy-done), custom_call_target="tpu_custom_call" | custom-call | tf_op jit(solution)/shard_map/combine/pallas_call | solution.py:395
Async XLA Ops:
  0.0 91.1 %copy-start = (f32[1,1,5,8,2,128,128]{6,5,4,3,2,1,0:T(8,128)S(1)}, f32[1,1,5,8,2,128,128]{6,5,4,3,2,1,0:T(8,128)}, u32[]{:S(2)}) copy-start(f32[1,1,5,8,2,128,128]{6,5,4,3,2,1,0:T(8,128)} %old_ref.1) | copy-start | bytes 15728644
  0.0 91.2 %copy-start.1 = (s32[1,1,5,128,5]{3,1,4,2,0:T(1,128)S(1)}, s32[1,1,5,128,5]{3,1,4,2,0:T(1,128)}, u32[]{:S(2)}) copy-start(s32[1,1,5,128,5]{3,1,4,2,0:T(1,128)} %param.6) | copy-start | bytes 38404
  0.0 91.2 %copy-start.2 = (s32[1,1,5]{2,1,0:T(1,128)S(1)}, s32[1,1,5]{2,1,0:T(1,128)}, u32[]{:S(2)}) copy-start(s32[1,1,5]{2,1,0:T(1,128)} %param.5) | copy-start | bytes 64

commit v2 on v1

v2 whole, which is shorter than its diff:
```python
import functools
import math

import jax
import jax.numpy as jnp
from jax import lax
from jax.experimental import pallas as pl
from jax.experimental.pallas import tpu as pltpu
from jax.sharding import PartitionSpec as P

EPSILON = 1e-06
MESH = pl.DeviceIdType.MESH
FLAG_BITS = 30


def whiten_rows(ref, index, first, count):
    segments, parts, _, width = ref.shape[len(index):]
    chunk = 16

    def rows(i, _):
        at = pl.ds(pl.multiple_of(first + i * chunk, chunk), chunk)
        pieces = [ref[(*index, s, p, at)].astype(jnp.float32)
                  for s in range(segments) for p in range(parts)]
        total = pieces[0] * pieces[0]
        for v in pieces[1:]:
            total = total + v * v
        power = jnp.sum(total, axis=1, keepdims=True) * (1.0 / (len(pieces) * width))
        scale = lax.rsqrt(power + EPSILON)
        for s in range(segments):
            for p in range(parts):
                ref[(*index, s, p, at)] = (pieces[s * parts + p] * scale).astype(jnp.bfloat16)
        return 0

    lax.fori_loop(0, count // chunk, rows, 0, unroll=2)


def product(left, right, scale):
    segments = left.count
    total = None
    for s in range(segments):
        part = lax.dot_general(
            left(s), right(s), (((1,), (1,)), ((), ())), preferred_element_type=jnp.float32
        )
        total = part if total is None else total + part
    n = total.shape[0] // 2
    real = total[:n, :n] + total[n:, n:]
    imag = total[n:, :n] - total[:n, n:]
    return real * scale, imag * scale


class View:
    def __init__(self, ref, index, count):
        self.ref, self.index, self.count = ref, index, count

    def __call__(self, s):
        v = self.ref[(*self.index, s)]
        return v.reshape(v.shape[0] * v.shape[1], v.shape[2])


OTHER = 3
PIECES = 4
AHEAD = 4
ACROSS = (1, 5, 7)
ORDER = (1, 5, 7, 0, 4, 6, 2, 3)
GROUP = (3, 0, 6, 6, 4, 1, 5, 2)


def cross_kernel(rows, cols, x_ref, self_ref, c_ref, both, stage,
                 first_sem, load_sem, xs, xr, zs, zr, ms, mr, ks, kr, rs, rr):
    blk, far = both.at[0], both.at[1]
    half, segments, stations, width = both.shape[1], both.shape[3], both.shape[5], both.shape[6]
    scale = 1.0 / math.sqrt(segments * width)
    piece = stations // PIECES
    turns = [(half + 1 - parity) // 2 for parity in (0, 1)]
    r = lax.axis_index("gx")
    c = lax.axis_index("gy")
    odd = lax.rem(c, 2)
    mate = c + 1 - 2 * odd
    keep_slot = 2 * odd
    halo_slot = 2 - 2 * odd
    z_to = c - 2 + 4 * odd
    z_from = c + 2 - 4 * odd
    sends_z = (z_to >= 0) & (z_to < cols)
    has_halo = (z_from >= 0) & (z_from < cols)
    first_col = c - 2 * odd
    above = r > 0
    below = r + 1 < rows
    left_pair = (odd == 0) | has_halo
    right_pair = (odd == 1) | has_halo

    def strip(q):
        return pl.ds(q * piece if isinstance(q, int) else pl.multiple_of(q * piece, piece), piece)

    def bins(b, mine):
        band = half * (odd if mine else 1 - odd) + b
        return pl.ds(pl.multiple_of(band * width, width), width)

    def load(b, mine):
        slot = keep_slot if mine else OTHER
        return pltpu.make_async_copy(
            x_ref.at[0, 0, :, :, :, bins(b, mine)], blk.at[b, slot], load_sem.at[int(mine), b])

    def load_first(q):
        return pltpu.make_async_copy(
            x_ref.at[0, 0, :, :, strip(q), bins(0, False)], blk.at[0, OTHER, :, :, strip(q)],
            first_sem.at[q])

    def x_copy(b, q):
        return pltpu.make_async_remote_copy(
            src_ref=blk.at[b, OTHER, :, :, strip(q)], dst_ref=blk.at[b, 1, :, :, strip(q)],
            send_sem=xs.at[0], recv_sem=xr.at[b, q],
            device_id=(r, mate), device_id_type=MESH)

    def z_copy(b):
        return pltpu.make_async_remote_copy(
            src_ref=blk.at[b, keep_slot], dst_ref=blk.at[b, halo_slot],
            send_sem=zs.at[0], recv_sem=zr.at[b], device_id=(r, z_to), device_id_type=MESH)

    def mid_copy(b, q, d):
        return pltpu.make_async_remote_copy(
            src_ref=blk.at[b, 1, :, :, strip(q)], dst_ref=far.at[b, d, :, :, strip(q)],
            send_sem=ms.at[d], recv_sem=mr.at[b, d],
            device_id=(r + 1 - 2 * d, c), device_id_type=MESH)

    def side_to(parity):
        return r - 1 + 2 * parity

    def sides(parity):
        to = side_to(parity)
        return (to >= 0) & (to < rows)

    def meets(parity):
        other_row = r + 1 - 2 * parity
        return (other_row >= 0) & (other_row < rows)

    def side_copy(parity, step):
        b = 2 * (step // (2 * PIECES)) + parity
        e = lax.rem(step // PIECES, 2)
        q = lax.rem(step, PIECES)
        slot = keep_slot + e * (OTHER - keep_slot)
        return pltpu.make_async_remote_copy(
            src_ref=blk.at[b, slot, :, :, strip(q)], dst_ref=far.at[b, 2 + e, :, :, strip(q)],
            send_sem=ks.at[parity], recv_sem=kr.at[b],
            device_id=(side_to(parity), c), device_id_type=MESH)

    def whole(slots, send, recv):
        return pltpu.make_async_remote_copy(
            src_ref=slots, dst_ref=slots, send_sem=send, recv_sem=recv,
            device_id=(r, mate), device_id_type=MESH)

    def r_copy(b, which, code, band, row, col):
        return pltpu.make_async_remote_copy(
            src_ref=stage.at[b, which], dst_ref=c_ref.at[code - 1, band],
            send_sem=rs.at[GROUP[which]], recv_sem=rr.at[code - 1],
            device_id=(row, col), device_id_type=MESH)

    def results(count, send=0, code=1):
        return whole(c_ref.at[0, pl.ds(0, count)], rs.at[send], rr.at[code - 1])

    def load_band(b, _):
        pl.when(b > 0)(load(b, False).start)
        load(b, True).start()
        return 0

    def send_other(b):
        load(b, False).wait()
        whiten_rows(both, (0, b, OTHER), 0, stations)
        for q in range(PIECES):
            x_copy(b, q).start()

    def send_mine(b, _):
        load(b, True).wait()
        whiten_rows(both, (0, b, keep_slot), 0, stations)
        pl.when(sends_z)(z_copy(b).start)
        return 0

    for q in range(PIECES):
        load_first(q).start()
    barrier = pltpu.get_barrier_semaphore()
    peers = jnp.int32(0)
    for dr in (0, 1, -1):
        for col in (mate, c - 2, c + 2) if dr == 0 else (c, mate):
            there = (r + dr >= 0) & (r + dr < rows) & (col >= 0) & (col < cols)
            peers = peers + there.astype(jnp.int32)

            @pl.when(there)
            def _():
                pl.semaphore_signal(barrier, inc=1, device_id=(r + dr, col), device_id_type=MESH)
    lax.fori_loop(0, half, load_band, 0)
    for q in range(PIECES):
        load_first(q).wait()
        whiten_rows(both, (0, 0, OTHER), q * piece, piece)
        if q == 0:
            pl.semaphore_wait(barrier, peers)
        x_copy(0, q).start()
    lax.fori_loop(0, 2, send_mine, 0)
    for step in range(AHEAD):
        for parity in (0, 1):
            pl.when(sides(parity))(side_copy(parity, jnp.int32(step)).start)

    def send_rest(b, _):
        send_other(b)

        @pl.when(b > 1)
        def _():
            send_mine(b, 0)
        return 0

    lax.fori_loop(1, half, send_rest, 0)

    def own_product(b):
        for slot, band in ((keep_slot, half * odd + b), (OTHER, half * (1 - odd) + b)):
            view = View(both, (0, b, slot), segments)
            real, imag = product(view, view, scale)
            self_ref[band, 0] = real
            self_ref[band, 1] = imag

    def routes(b):
        is_odd = lax.rem(b, 2)
        even = is_odd == 0
        band, other_band = half * odd + b, half * (1 - odd) + b
        near = odd == 0
        left, mid, right = (0, b, 0), (0, b, 1), (0, b, 2)
        mid_above, mid_below = (1, b, 0), (1, b, 1)
        keeps = (is_odd, b, keep_slot + is_odd * (2 - keep_slot)), (1 - is_odd, b, 2 + is_odd * (keep_slot - 2))
        return [
            (0, left, mid, 3, band, r, first_col, left_pair, near),
            (1, mid, right, 3, band, r, mate, right_pair, None),
            (2, *keeps, 1, band, r - is_odd, c, meets(is_odd), even),
            (3, (is_odd, b, OTHER), (1 - is_odd, b, OTHER), 1, other_band, r - is_odd, c, meets(is_odd), even),
            (4, left, mid_below, 4, band, r, first_col, below & left_pair, near),
            (5, mid_above, right, 4, band, r - 1, mate, above & right_pair, None),
            (6, left, mid_above, 2, band, r, first_col, above & left_pair, near),
            (7, mid_below, right, 2, band, r + 1, mate, below & right_pair, None),
        ]

    def emit(b, route, go=True):
        which, left, right, code, band, row, col, present, local = route

        @pl.when(present)
        def _():
            real, imag = product(View(both, left, segments), View(both, right, segments), scale)
            real, imag = real.astype(jnp.bfloat16), imag.astype(jnp.bfloat16)

            def remote():
                stage[b, which, 0] = real
                stage[b, which, 1] = imag
                pl.when(go)(r_copy(b, which, code, band, row, col).start)

            if local is None:
                remote()
            else:
                @pl.when(local)
                def _():
                    c_ref[code - 1, band, 0] = real
                    c_ref[code - 1, band, 1] = imag

                pl.when(jnp.logical_not(local))(remote)

    def fire(a):
        table = routes(a)
        for which in ACROSS:
            _, _, _, code, band, row, col, present, _ = table[which]
            pl.when(present)(r_copy(a, which, code, band, row, col).start)

    def step(b, _):
        for q in range(PIECES):
            @pl.when(b < half)
            def _():
                if q == 3:
                    @pl.when(b == half - 1)
                    def _():
                        for a in range(half - 1):
                            fire(a)
                x_copy(b, q).wait_recv()
                for d, there in ((0, below), (1, above)):
                    pl.when(there)(mid_copy(b, q, d).start)
                at = b * PIECES + q + AHEAD
                for parity in (0, 1):
                    pl.when(sides(parity) & (at < 2 * PIECES * turns[parity]))(side_copy(parity, at).start)

            @pl.when(b == 0)
            def _():
                for a in range(q, half, PIECES):
                    own_product(a)

            @pl.when(b > 0)
            def _():
                a = b - 1
                table = routes(a)
                for which in ORDER[2 * q: 2 * q + 2]:
                    if which == 1:
                        pl.when(has_halo)(z_copy(a).wait_recv)
                    if which == 5:
                        pl.when(above)(whole(far.at[a, 0], ms.at[0], mr.at[a, 0]).wait_recv)
                    if which == 7:
                        pl.when(below)(whole(far.at[a, 1], ms.at[0], mr.at[a, 1]).wait_recv)
                    if which == 2:
                        pl.when(meets(lax.rem(a, 2)))(
                            whole(far.at[a, pl.ds(2, 2)], ks.at[0], kr.at[a]).wait_recv)
                    emit(a, table[which], a == half - 1 if which in ACROSS else True)
        return 0

    lax.fori_loop(0, half + 1, step, 0)

    whole(blk.at[:, OTHER], xs.at[0], xr.at[0, 0]).wait_send()
    pl.when(sends_z)(whole(blk.at[:, OTHER], zs.at[0], xr.at[0, 0]).wait_send)
    for d, there in ((0, below), (1, above)):
        pl.when(there)(whole(blk.at[:, 1], ms.at[d], xr.at[0, 0]).wait_send)
    for parity in (0, 1):
        pl.when(sides(parity))(
            whole(far.at[pl.ds(0, turns[parity]), pl.ds(2, 2)], ks.at[parity], xr.at[0, 0]).wait_send)
    for group, there in enumerate((right_pair, above & right_pair, below & right_pair)):
        pl.when(there)(results(half, group).wait_send)
    for group, there in enumerate((left_pair, below & left_pair, above & left_pair), 3):
        pl.when(there & (odd == 1))(results(half, group).wait_send)
    pl.when(meets(1))(results(2 * turns[1], 6).wait_send)

    next_col = c + 1 < cols
    pl.when(below)(results(2 * turns[1], code=1).wait_recv)
    for code, comes in ((2, above & next_col), (3, next_col), (4, below & next_col)):
        pl.when(comes & (odd == 1))(results(2 * half, code=code).wait_recv)
        pl.when(comes & (odd == 0))(results(half, code=code).wait_recv)


def crosses(spectra, bands, rows, cols):
    segments, parts, stations, bins = spectra.shape[2:]
    half, width = bands // 2, bins // bands
    dma = pltpu.SemaphoreType.DMA
    return pl.pallas_call(
        functools.partial(cross_kernel, rows, cols),
        out_shape=(
            jax.ShapeDtypeStruct((bands, 2, stations, stations), jnp.float32),
            jax.ShapeDtypeStruct((4, bands, 2, stations, stations), jnp.bfloat16),
        ),
        in_specs=[pl.BlockSpec(memory_space=pltpu.MemorySpace.HBM)],
        out_specs=(pl.BlockSpec(memory_space=pltpu.VMEM), pl.BlockSpec(memory_space=pltpu.VMEM)),
        scratch_shapes=[
            pltpu.VMEM((2, half, 4, segments, parts, stations, width), jnp.bfloat16),
            pltpu.VMEM((half, 8, 2, stations, stations), jnp.bfloat16),
            dma((PIECES,)), dma((2, half)),
            dma((1,)), dma((half, PIECES)),
            dma((1,)), dma((half,)),
            dma((2,)), dma((half, 2)),
            dma((2,)), dma((half,)),
            dma((7,)), dma((4,)),
        ],
        compiler_params=pltpu.CompilerParams(collective_id=0, has_side_effects=True, vmem_limit_bytes=48 * 1024 * 1024),
        name="crosses",
    )(spectra)


def combine_kernel(codes, self_ref, c_ref, bits_ref, old_ref, out_ref, done, sem):
    slots, bands = old_ref.shape[2:4]
    words, stations = bits_ref.shape[2], bits_ref.shape[4]
    column = lax.broadcasted_iota(jnp.int32, (stations, stations), 0)

    def write(s):
        return pltpu.make_async_copy(done.at[s], out_ref.at[0, 0, s], sem.at[s])

    for s in range(slots):
        code = codes[s]
        chosen = jnp.zeros((stations, stations), jnp.int32)
        bit = column
        for w in range(words):
            reached = column >= w * FLAG_BITS
            chosen = jnp.where(reached, bits_ref[0, s, w], chosen)
            bit = jnp.where(reached, column - w * FLAG_BITS, bit)
        flags = jnp.bitwise_and(jnp.right_shift(chosen, bit), 1).astype(jnp.float32).T > 0.5

        @pl.when(code == 0)
        def _():
            for k in range(bands):
                done[s, k] = old_ref[0, 0, s, k] + jnp.where(flags, self_ref[k], 0.0)

        @pl.when(code > 0)
        def _():
            for k in range(bands):
                done[s, k] = old_ref[0, 0, s, k] + jnp.where(
                    flags, c_ref[code - 1, k].astype(jnp.float32), 0.0)

        @pl.when(code < 0)
        def _():
            done[s] = old_ref[0, 0, s]

        write(s).start()
    for s in range(slots):
        write(s).wait()


def combine(codes, own, cross, range_bits, old):
    slots, bands, parts, stations = old.shape[2:6]
    vmem = pl.BlockSpec(memory_space=pltpu.VMEM)
    return pl.pallas_call(
        combine_kernel,
        out_shape=jax.ShapeDtypeStruct(old.shape, old.dtype),
        in_specs=[pl.BlockSpec(memory_space=pltpu.SMEM), vmem, vmem, vmem, vmem],
        out_specs=pl.BlockSpec(memory_space=pltpu.MemorySpace.HBM),
        scratch_shapes=[
            pltpu.VMEM((slots, bands, parts, stations, stations), jnp.float32),
            pltpu.SemaphoreType.DMA((slots,)),
        ],
        compiler_params=pltpu.CompilerParams(vmem_limit_bytes=20 * 1024 * 1024),
        name="combine",
    )(codes, own, cross, jnp.transpose(range_bits, (0, 2, 4, 1, 3)), old)


def solution(mesh):
    rows, cols = mesh.shape["gx"], mesh.shape["gy"]

    def body(spectra, partner_codes, range_bits, old_stacks):
        own, cross = crosses(spectra, old_stacks.shape[3], rows, cols)
        return combine(partner_codes[0, 0], own, cross, range_bits, old_stacks)

    return jax.shard_map(
        body,
        mesh=mesh,
        in_specs=(
            P("gx", "gy", None, None, None, None),
            P("gx", "gy", None),
            P("gx", "gy", None, None, None),
            P("gx", "gy", None, None, None, None, None),
        ),
        out_specs=P("gx", "gy", None, None, None, None, None),
        check_vma=False,
    )
```

time: 94.5 us -> 90.2 us (0.954); the launches traced: 94.3 us -> 88.5 us
  Pallas kernels: 94.3 us -> 88.5 us
    pallas_call x1, Pallas kernels: 91.1 us -> 85.3 us  [crosses(): pl.pallas_call(functools.partial(cross_kernel, rows, cols), out_shape=(ja...]
where the time goes in v2:
time: 90.2 us; the launch traced here: 88.5 us
  Pallas kernels  88.5 us (98%)
    pallas_call x1, Pallas kernels, crosses(): pl.pallas_call(functools.partial(cross_kernel, rows, cols), out_shape=(ja...  85.3 us
    pallas_call x1, Pallas kernels, combine(): pl.pallas_call(combine_kernel, out_shape=jax.ShapeDtypeStruct(old.shape,...  3.14 us

profile of v2, /device:TPU:11, one launch (start us, length us, event | category | flops | bytes accessed | tf_op | source)
XLA Modules:
  0.0 88.5 jit_solution(6877187108878607925)
XLA Ops:
  0.0 0.0 copy-start
  0.0 0.0 copy-start.1
  0.0 0.0 copy-start.2
  0.0 85.3 %crosses.1 = (f32[8,2,128,128]{3,2,1,0:T(8,128)S(1)}, bf16[4,8,2,128,128]{4,3,2,1,0:T(8,128)(2,1)S(1)}) custom-call(bf16[1,1,3,2,128,4096]{5,4,3,2,1,0:T(8,128)(2,1)} %x_ref.1), custom_call_target="tpu_custom_call" | custom-call | tf_op jit(solution)/shard_map/crosses/pallas_call | solution.py:330
  85.4 0.0 copy-done
  85.4 0.0 copy-done.1
  85.4 0.0 copy-done.2
  85.4 3.1 %combine.1 = f32[1,1,5,8,2,128,128]{6,5,4,3,2,1,0:T(8,128)} custom-call(s32[5]{0:T(128)S(1)} %bitcast.3, f32[8,2,128,128]{3,2,1,0:T(8,128)S(1)} %get-tuple-element.7.self_ref, bf16[4,8,2,128,128]{4,3,2,1,0:T(8,128)(2,1)S(1)} %get-tuple-element.8.c_ref, s32[1,5,5,1,128]{4,3,2,1,0:T(1,128)S(1)} %bitcast.2, f32[1,1,5,8,2,128,128]{6,5,4,3,2,1,0:T(8,128)S(1)} %copy-done), custom_call_target="tpu_custom_call" | custom-call | tf_op jit(solution)/shard_map/combine/pallas_call | solution.py:394
Async XLA Ops:
  0.0 85.4 %copy-start = (f32[1,1,5,8,2,128,128]{6,5,4,3,2,1,0:T(8,128)S(1)}, f32[1,1,5,8,2,128,128]{6,5,4,3,2,1,0:T(8,128)}, u32[]{:S(2)}) copy-start(f32[1,1,5,8,2,128,128]{6,5,4,3,2,1,0:T(8,128)} %old_ref.1) | copy-start | bytes 15728644
  0.0 85.4 %copy-start.1 = (s32[1,1,5,128,5]{3,1,4,2,0:T(1,128)S(1)}, s32[1,1,5,128,5]{3,1,4,2,0:T(1,128)}, u32[]{:S(2)}) copy-start(s32[1,1,5,128,5]{3,1,4,2,0:T(1,128)} %param.6) | copy-start | bytes 38404
  0.0 85.4 %copy-start.2 = (s32[1,1,5]{2,1,0:T(1,128)S(1)}, s32[1,1,5]{2,1,0:T(1,128)}, u32[]{:S(2)}) copy-start(s32[1,1,5]{2,1,0:T(1,128)} %param.5) | copy-start | bytes 64

commit v3 on v2

--- a/solution.py
+++ b/solution.py
@@ -59,6 +59,7 @@
 
 OTHER = 3
 PIECES = 4
+EARLY = 1
 AHEAD = 4
 ACROSS = (1, 5, 7)
 ORDER = (1, 5, 7, 0, 4, 6, 2, 3)
@@ -257,11 +258,14 @@
 
                 pl.when(jnp.logical_not(local))(remote)
 
-    def fire(a):
+    last = jnp.where(lax.rem(r, 2) == 0, 1, jnp.where((r == 1) & (c == 1), 7, 5))
+
+    def fire(a, held):
         table = routes(a)
         for which in ACROSS:
             _, _, _, code, band, row, col, present, _ = table[which]
-            pl.when(present)(r_copy(a, which, code, band, row, col).start)
+            turn = (last == which) == held
+            pl.when(present & turn)(r_copy(a, which, code, band, row, col).start)
 
     def step(b, _):
         for q in range(PIECES):
@@ -271,7 +275,9 @@
                     @pl.when(b == half - 1)
                     def _():
                         for a in range(half - 1):
-                            fire(a)
+                            fire(a, False)
+                        for a in range(EARLY):
+                            fire(a, True)
                 x_copy(b, q).wait_recv()
                 for d, there in ((0, below), (1, above)):
                     pl.when(there)(mid_copy(b, q, d).start)
@@ -298,7 +304,12 @@
                     if which == 2:
                         pl.when(meets(lax.rem(a, 2)))(
                             whole(far.at[a, pl.ds(2, 2)], ks.at[0], kr.at[a]).wait_recv)
-                    emit(a, table[which], a == half - 1 if which in ACROSS else True)
+                    emit(a, table[which], (a == half - 1) & (last != which) if which in ACROSS else True)
+                    if which == 7:
+                        @pl.when(a == half - 1)
+                        def _():
+                            for e in range(EARLY, half):
+                                fire(e, True)
         return 0
 
     lax.fori_loop(0, half + 1, step, 0)
@@ -350,42 +361,58 @@
     )(spectra)
 
 
-def combine_kernel(codes, self_ref, c_ref, bits_ref, old_ref, out_ref, done, sem):
+def combine_kernel(codes_ref, self_ref, c_ref, bits_ref, old_ref, out_ref, done, flags_ref, codes, code_sem, sem):
     slots, bands = old_ref.shape[2:4]
     words, stations = bits_ref.shape[2], bits_ref.shape[4]
     column = lax.broadcasted_iota(jnp.int32, (stations, stations), 0)
-
-    def write(s):
-        return pltpu.make_async_copy(done.at[s], out_ref.at[0, 0, s], sem.at[s])
-
-    for s in range(slots):
-        code = codes[s]
+    span = bands // 2
+
+    def write(s, first=0, count=bands):
+        at = pl.ds(first, count)
+        return pltpu.make_async_copy(done.at[s, at], out_ref.at[0, 0, s, at], sem)
+
+    def near(s):
         chosen = jnp.zeros((stations, stations), jnp.int32)
         bit = column
         for w in range(words):
             reached = column >= w * FLAG_BITS
             chosen = jnp.where(reached, bits_ref[0, s, w], chosen)
             bit = jnp.where(reached, column - w * FLAG_BITS, bit)
-        flags = jnp.bitwise_and(jnp.right_shift(chosen, bit), 1).astype(jnp.float32).T > 0.5
-
-        @pl.when(code == 0)
-        def _():
-            for k in range(bands):
-                done[s, k] = old_ref[0, 0, s, k] + jnp.where(flags, self_ref[k], 0.0)
-
-        @pl.when(code > 0)
-        def _():
-            for k in range(bands):
-                done[s, k] = old_ref[0, 0, s, k] + jnp.where(
-                    flags, c_ref[code - 1, k].astype(jnp.float32), 0.0)
-
-        @pl.when(code < 0)
-        def _():
-            done[s] = old_ref[0, 0, s]
-
+        return jnp.bitwise_and(jnp.right_shift(chosen, bit), 1).astype(jnp.float32).T > 0.5
+
+    fetch = pltpu.make_async_copy(codes_ref, codes, code_sem)
+    fetch.start()
+    flags = near(0)
+    for h in range(2):
+        def own(k, _):
+            done[0, k] = old_ref[0, 0, 0, k] + jnp.where(flags, self_ref[k], 0.0)
+            return 0
+
+        lax.fori_loop(h * span, (h + 1) * span, own, 0)
+        write(0, h * span, span).start()
+
+    def unpack(s, _):
+        flags_ref[s] = near(s).astype(jnp.float32)
+        return 0
+
+    lax.fori_loop(1, slots, unpack, 0)
+    fetch.wait()
+
+    def slot(s, _):
+        code = codes[s]
+        flags = (flags_ref[s] > 0.5) & (code > 0)
+        at = jnp.maximum(code - 1, 0)
+
+        def band(k, _):
+            done[s, k] = old_ref[0, 0, s, k] + jnp.where(flags, c_ref[at, k].astype(jnp.float32), 0.0)
+            return 0
+
+        lax.fori_loop(0, bands, band, 0)
         write(s).start()
-    for s in range(slots):
-        write(s).wait()
+        return 0
+
+    lax.fori_loop(1, slots, slot, 0)
+    pltpu.make_async_copy(done, out_ref.at[0, 0], sem).wait()
 
 
 def combine(codes, own, cross, range_bits, old):
@@ -394,11 +421,14 @@
     return pl.pallas_call(
         combine_kernel,
         out_shape=jax.ShapeDtypeStruct(old.shape, old.dtype),
-        in_specs=[pl.BlockSpec(memory_space=pltpu.SMEM), vmem, vmem, vmem, vmem],
+        in_specs=[vmem] * 5,
         out_specs=pl.BlockSpec(memory_space=pltpu.MemorySpace.HBM),
         scratch_shapes=[
             pltpu.VMEM((slots, bands, parts, stations, stations), jnp.float32),
-            pltpu.SemaphoreType.DMA((slots,)),
+            pltpu.VMEM((slots, stations, stations), jnp.float32),
+            pltpu.SMEM(codes.shape, jnp.int32),
+            pltpu.SemaphoreType.DMA(()),
+            pltpu.SemaphoreType.DMA(()),
         ],
         compiler_params=pltpu.CompilerParams(vmem_limit_bytes=20 * 1024 * 1024),
         name="combine",

time: 90.2 us -> 89.1 us (0.988)
  Pallas kernels: 88.5 us -> 87.4 us
where the time goes in v3:
time: 89.1 us; the launch traced here: 87.4 us
  Pallas kernels  87.4 us (98%)
    pallas_call x1, Pallas kernels, crosses(): pl.pallas_call(functools.partial(cross_kernel, rows, cols), out_shape=(ja...  84.5 us
    pallas_call x1, Pallas kernels, combine(): pl.pallas_call(combine_kernel, out_shape=jax.ShapeDtypeStruct(old.shape,...  2.86 us

profile of v3, /device:TPU:11, one launch (start us, length us, event | category | flops | bytes accessed | tf_op | source)
XLA Modules:
  0.0 87.4 jit_solution(6888746079256102671)
XLA Ops:
  0.0 0.0 copy-start
  0.0 0.0 copy-start.1
  0.0 0.0 copy-start.2
  0.0 84.5 %crosses.1 = (f32[8,2,128,128]{3,2,1,0:T(8,128)S(1)}, bf16[4,8,2,128,128]{4,3,2,1,0:T(8,128)(2,1)S(1)}) custom-call(bf16[1,1,3,2,128,4096]{5,4,3,2,1,0:T(8,128)(2,1)} %x_ref.1), custom_call_target="tpu_custom_call" | custom-call | tf_op jit(solution)/shard_map/crosses/pallas_call | solution.py:341
  84.5 0.0 copy-done
  84.6 0.0 copy-done.1
  84.6 0.0 copy-done.2
  84.6 2.9 %combine.1 = f32[1,1,5,8,2,128,128]{6,5,4,3,2,1,0:T(8,128)} custom-call(s32[5]{0:T(128)S(1)} %bitcast.3, f32[8,2,128,128]{3,2,1,0:T(8,128)S(1)} %get-tuple-element.7.self_ref, bf16[4,8,2,128,128]{4,3,2,1,0:T(8,128)(2,1)S(1)} %get-tuple-element.8.c_ref, s32[1,5,5,1,128]{4,3,2,1,0:T(1,128)S(1)} %bitcast.2, f32[1,1,5,8,2,128,128]{6,5,4,3,2,1,0:T(8,128)S(1)} %copy-done), custom_call_target="tpu_custom_call" | custom-call | tf_op jit(solution)/shard_map/combine/pallas_call | solution.py:421
Async XLA Ops:
  0.0 84.5 %copy-start = (f32[1,1,5,8,2,128,128]{6,5,4,3,2,1,0:T(8,128)S(1)}, f32[1,1,5,8,2,128,128]{6,5,4,3,2,1,0:T(8,128)}, u32[]{:S(2)}) copy-start(f32[1,1,5,8,2,128,128]{6,5,4,3,2,1,0:T(8,128)} %old_ref.1) | copy-start | bytes 15728644
  0.0 84.5 %copy-start.1 = (s32[1,1,5,128,5]{3,1,4,2,0:T(1,128)S(1)}, s32[1,1,5,128,5]{3,1,4,2,0:T(1,128)}, u32[]{:S(2)}) copy-start(s32[1,1,5,128,5]{3,1,4,2,0:T(1,128)} %param.6) | copy-start | bytes 38404
  0.0 84.6 %copy-start.2 = (s32[1,1,5]{2,1,0:T(1,128)S(1)}, s32[1,1,5]{2,1,0:T(1,128)}, u32[]{:S(2)}) copy-start(s32[1,1,5]{2,1,0:T(1,128)} %param.5) | copy-start | bytes 64

commit v4 on v3

--- a/solution.py
+++ b/solution.py
@@ -66,8 +66,16 @@
 GROUP = (3, 0, 6, 6, 4, 1, 5, 2)
 
 
-def cross_kernel(rows, cols, x_ref, self_ref, c_ref, both, stage,
-                 first_sem, load_sem, xs, xr, zs, zr, ms, mr, ks, kr, rs, rr):
+def codes_of(slot):
+    return range(slot, 5) if slot else ()
+
+
+def place(slot, code):
+    return 1 + sum(len(codes_of(s)) for s in range(slot)) + code - slot
+
+
+def cross_kernel(rows, cols, x_ref, codes_ref, bits_ref, old_ref, own_ref, chosen_ref, c_ref, both, stage,
+                 bits, codes, side_sem, first_sem, load_sem, xs, xr, zs, zr, ms, mr, ks, kr, rs, rr):
     blk, far = both.at[0], both.at[1]
     half, segments, stations, width = both.shape[1], both.shape[3], both.shape[5], both.shape[6]
     scale = 1.0 / math.sqrt(segments * width)
@@ -158,6 +166,32 @@
     def results(count, send=0, code=1):
         return whole(c_ref.at[0, pl.ds(0, count)], rs.at[send], rr.at[code - 1])
 
+    def load_codes():
+        return pltpu.make_async_copy(codes_ref, codes, side_sem.at[0])
+
+    def load_bits():
+        return pltpu.make_async_copy(bits_ref.at[0], bits, side_sem.at[1])
+
+    def load_old():
+        return pltpu.make_async_copy(old_ref.at[0, 0, 0], own_ref, side_sem.at[2])
+
+    def unpack():
+        column = lax.broadcasted_iota(jnp.int32, (stations, stations), 0)
+        load_bits().wait()
+        load_codes().wait()
+        for s in range(bits.shape[0]):
+            word = jnp.zeros((stations, stations), jnp.int32)
+            bit = column
+            for w in range(bits.shape[1]):
+                reached = column >= w * FLAG_BITS
+                word = jnp.where(reached, bits[s, w], word)
+                bit = jnp.where(reached, column - w * FLAG_BITS, bit)
+            near = jnp.bitwise_and(jnp.right_shift(word, bit), 1).astype(jnp.float32).T
+            if s == 0:
+                chosen_ref[0] = near
+            for code in codes_of(s):
+                chosen_ref[place(s, code)] = near * jnp.where(codes[s] == code, 1.0, 0.0)
+
     def load_band(b, _):
         pl.when(b > 0)(load(b, False).start)
         load(b, True).start()
@@ -188,6 +222,9 @@
             def _():
                 pl.semaphore_signal(barrier, inc=1, device_id=(r + dr, col), device_id_type=MESH)
     lax.fori_loop(0, half, load_band, 0)
+    load_codes().start()
+    load_bits().start()
+    load_old().start()
     for q in range(PIECES):
         load_first(q).wait()
         whiten_rows(both, (0, 0, OTHER), q * piece, piece)
@@ -213,8 +250,9 @@
         for slot, band in ((keep_slot, half * odd + b), (OTHER, half * (1 - odd) + b)):
             view = View(both, (0, b, slot), segments)
             real, imag = product(view, view, scale)
-            self_ref[band, 0] = real
-            self_ref[band, 1] = imag
+            near = chosen_ref[0] > 0.5
+            own_ref[band, 0] += jnp.where(near, real, 0.0)
+            own_ref[band, 1] += jnp.where(near, imag, 0.0)
 
     def routes(b):
         is_odd = lax.rem(b, 2)
@@ -312,6 +350,8 @@
                                 fire(e, True)
         return 0
 
+    unpack()
+    load_old().wait()
     lax.fori_loop(0, half + 1, step, 0)
 
     whole(blk.at[:, OTHER], xs.at[0], xr.at[0, 0]).wait_send()
@@ -334,22 +374,29 @@
         pl.when(comes & (odd == 0))(results(half, code=code).wait_recv)
 
 
-def crosses(spectra, bands, rows, cols):
+def crosses(spectra, codes, range_bits, old, rows, cols):
     segments, parts, stations, bins = spectra.shape[2:]
+    slots, bands, words = old.shape[2], old.shape[3], range_bits.shape[4]
     half, width = bands // 2, bins // bands
+    hbm = pl.BlockSpec(memory_space=pltpu.MemorySpace.HBM)
+    vmem = pl.BlockSpec(memory_space=pltpu.VMEM)
+    bits = jnp.transpose(range_bits, (0, 2, 4, 1, 3))
     dma = pltpu.SemaphoreType.DMA
     return pl.pallas_call(
         functools.partial(cross_kernel, rows, cols),
         out_shape=(
             jax.ShapeDtypeStruct((bands, 2, stations, stations), jnp.float32),
+            jax.ShapeDtypeStruct((place(slots, slots), stations, stations), jnp.float32),
             jax.ShapeDtypeStruct((4, bands, 2, stations, stations), jnp.bfloat16),
         ),
-        in_specs=[pl.BlockSpec(memory_space=pltpu.MemorySpace.HBM)],
-        out_specs=(pl.BlockSpec(memory_space=pltpu.VMEM), pl.BlockSpec(memory_space=pltpu.VMEM)),
+        in_specs=[hbm] * 4,
+        out_specs=(vmem, vmem, vmem),
         scratch_shapes=[
             pltpu.VMEM((2, half, 4, segments, parts, stations, width), jnp.bfloat16),
             pltpu.VMEM((half, 8, 2, stations, stations), jnp.bfloat16),
-            dma((PIECES,)), dma((2, half)),
+            pltpu.VMEM((slots, words, 1, stations), jnp.int32),
+            pltpu.SMEM(codes.shape, jnp.int32),
+            dma((3,)), dma((PIECES,)), dma((2, half)),
             dma((1,)), dma((half, PIECES)),
             dma((1,)), dma((half,)),
             dma((2,)), dma((half, 2)),
@@ -358,89 +405,56 @@
         ],
         compiler_params=pltpu.CompilerParams(collective_id=0, has_side_effects=True, vmem_limit_bytes=48 * 1024 * 1024),
         name="crosses",
-    )(spectra)
-
-
-def combine_kernel(codes_ref, self_ref, c_ref, bits_ref, old_ref, out_ref, done, flags_ref, codes, code_sem, sem):
+    )(
+        spectra,
+        pltpu.with_memory_space_constraint(codes, pltpu.HBM),
+        pltpu.with_memory_space_constraint(bits, pltpu.HBM),
+        old,
+    )
+
+
+def combine_kernel(own_ref, chosen_ref, c_ref, old_ref, out_ref, done, own_sem, sem):
     slots, bands = old_ref.shape[2:4]
-    words, stations = bits_ref.shape[2], bits_ref.shape[4]
-    column = lax.broadcasted_iota(jnp.int32, (stations, stations), 0)
-    span = bands // 2
-
-    def write(s, first=0, count=bands):
-        at = pl.ds(first, count)
-        return pltpu.make_async_copy(done.at[s, at], out_ref.at[0, 0, s, at], sem)
-
-    def near(s):
-        chosen = jnp.zeros((stations, stations), jnp.int32)
-        bit = column
-        for w in range(words):
-            reached = column >= w * FLAG_BITS
-            chosen = jnp.where(reached, bits_ref[0, s, w], chosen)
-            bit = jnp.where(reached, column - w * FLAG_BITS, bit)
-        return jnp.bitwise_and(jnp.right_shift(chosen, bit), 1).astype(jnp.float32).T > 0.5
-
-    fetch = pltpu.make_async_copy(codes_ref, codes, code_sem)
-    fetch.start()
-    flags = near(0)
-    for h in range(2):
-        def own(k, _):
-            done[0, k] = old_ref[0, 0, 0, k] + jnp.where(flags, self_ref[k], 0.0)
+    own = pltpu.make_async_copy(own_ref, out_ref.at[0, 0, 0], own_sem)
+    own.start()
+    for s in reversed(range(1, slots)):
+        def band(k, _):
+            total = old_ref[0, 0, s, k]
+            for code in codes_of(s):
+                near = chosen_ref[place(s, code)] > 0.5
+                total = total + jnp.where(near, c_ref[code - 1, k].astype(jnp.float32), 0.0)
+            done[s - 1, k] = total
             return 0
 
-        lax.fori_loop(h * span, (h + 1) * span, own, 0)
-        write(0, h * span, span).start()
-
-    def unpack(s, _):
-        flags_ref[s] = near(s).astype(jnp.float32)
-        return 0
-
-    lax.fori_loop(1, slots, unpack, 0)
-    fetch.wait()
-
-    def slot(s, _):
-        code = codes[s]
-        flags = (flags_ref[s] > 0.5) & (code > 0)
-        at = jnp.maximum(code - 1, 0)
-
-        def band(k, _):
-            done[s, k] = old_ref[0, 0, s, k] + jnp.where(flags, c_ref[at, k].astype(jnp.float32), 0.0)
-            return 0
-
         lax.fori_loop(0, bands, band, 0)
-        write(s).start()
-        return 0
-
-    lax.fori_loop(1, slots, slot, 0)
-    pltpu.make_async_copy(done, out_ref.at[0, 0], sem).wait()
-
-
-def combine(codes, own, cross, range_bits, old):
+        pltpu.make_async_copy(done.at[s - 1], out_ref.at[0, 0, s], sem).start()
+    own.wait()
+    pltpu.make_async_copy(done, out_ref.at[0, 0, pl.ds(1, slots - 1)], sem).wait()
+
+
+def combine(own, chosen, cross, old):
     slots, bands, parts, stations = old.shape[2:6]
-    vmem = pl.BlockSpec(memory_space=pltpu.VMEM)
     return pl.pallas_call(
         combine_kernel,
         out_shape=jax.ShapeDtypeStruct(old.shape, old.dtype),
-        in_specs=[vmem] * 5,
+        in_specs=[pl.BlockSpec(memory_space=pltpu.VMEM)] * 4,
         out_specs=pl.BlockSpec(memory_space=pltpu.MemorySpace.HBM),
         scratch_shapes=[
-            pltpu.VMEM((slots, bands, parts, stations, stations), jnp.float32),
-            pltpu.VMEM((slots, stations, stations), jnp.float32),
-            pltpu.SMEM(codes.shape, jnp.int32),
+            pltpu.VMEM((slots - 1, bands, parts, stations, stations), jnp.float32),
             pltpu.SemaphoreType.DMA(()),
             pltpu.SemaphoreType.DMA(()),
         ],
-        compiler_params=pltpu.CompilerParams(vmem_limit_bytes=20 * 1024 * 1024),
+        compiler_params=pltpu.CompilerParams(vmem_limit_bytes=16 * 1024 * 1024),
         name="combine",
-    )(codes, own, cross, jnp.transpose(range_bits, (0, 2, 4, 1, 3)), old)
+    )(own, chosen, cross, old)
 
 
 def solution(mesh):
     rows, cols = mesh.shape["gx"], mesh.shape["gy"]
 
     def body(spectra, partner_codes, range_bits, old_stacks):
-        own, cross = crosses(spectra, old_stacks.shape[3], rows, cols)
-        return combine(partner_codes[0, 0], own, cross, range_bits, old_stacks)
+        own, chosen, cross = crosses(spectra, partner_codes[0, 0], range_bits, old_stacks, rows, cols)
+        return combine(own, chosen, cross, old_stacks)
 
     return jax.shard_map(
         body,

time: 89.1 us -> 88.6 us (level)
  no operation moved by 1% of the time
where the time goes in v4:
time: 88.6 us; the launch traced here: 86.9 us
  Pallas kernels  86.9 us (98%)
    pallas_call x1, Pallas kernels, crosses(): pl.pallas_call(functools.partial(cross_kernel, rows, cols), out_shape=(ja...  84.5 us
    pallas_call x1, Pallas kernels, combine(): pl.pallas_call(combine_kernel, out_shape=jax.ShapeDtypeStruct(old.shape,...  2.4 us

profile of v4, /device:TPU:11, one launch (start us, length us, event | category | flops | bytes accessed | tf_op | source)
XLA Modules:
  0.0 86.9 jit_solution(3574774694755771188)
XLA Ops:
  0.0 0.0 copy-start
  0.0 84.5 %crosses.1 = (f32[8,2,128,128]{3,2,1,0:T(8,128)S(1)}, f32[11,128,128]{2,1,0:T(8,128)S(1)}, bf16[4,8,2,128,128]{4,3,2,1,0:T(8,128)(2,1)S(1)}) custom-call(bf16[1,1,3,2,128,4096]{5,4,3,2,1,0:T(8,128)(2,1)} %x_ref.1, s32[5]{0:T(128)} %bitcast.3, s32[1,5,5,1,128]{4,3,2,1,0:T(1,128)} %bitcast.2, f32[1,1,5,8,2,128,128]{6,5,4,3,2,1,0:T(8,128)} %old_ref.3), custom_call_target="tpu_custom_call" | custom-call | tf_op jit(solution)/shard_map/crosses/pallas_call | solution.py:385
  84.5 0.0 copy-done
  84.5 2.4 %combine.1 = f32[1,1,5,8,2,128,128]{6,5,4,3,2,1,0:T(8,128)} custom-call(f32[8,2,128,128]{3,2,1,0:T(8,128)S(1)} %get-tuple-element.8.own_ref, f32[11,128,128]{2,1,0:T(8,128)S(1)} %get-tuple-element.9.chosen_ref, bf16[4,8,2,128,128]{4,3,2,1,0:T(8,128)(2,1)S(1)} %get-tuple-element.10.c_ref, f32[1,1,5,8,2,128,128]{6,5,4,3,2,1,0:T(8,128)S(1)} %copy-done), custom_call_target="tpu_custom_call" | custom-call | tf_op jit(solution)/shard_map/combine/pallas_call | solution.py:437
Async XLA Ops:
  0.0 84.5 %copy-start = (f32[1,1,5,8,2,128,128]{6,5,4,3,2,1,0:T(8,128)S(1)}, f32[1,1,5,8,2,128,128]{6,5,4,3,2,1,0:T(8,128)}, u32[]{:S(2)}) copy-start(f32[1,1,5,8,2,128,128]{6,5,4,3,2,1,0:T(8,128)} %old_ref.3) | copy-start | bytes 15728644

commit v5 on v4

--- a/solution.py
+++ b/solution.py
@@ -60,7 +60,7 @@
 OTHER = 3
 PIECES = 4
 EARLY = 1
-AHEAD = 4
+AHEAD = 8
 ACROSS = (1, 5, 7)
 ORDER = (1, 5, 7, 0, 4, 6, 2, 3)
 GROUP = (3, 0, 6, 6, 4, 1, 5, 2)
@@ -75,7 +75,7 @@
 
 
 def cross_kernel(rows, cols, x_ref, codes_ref, bits_ref, old_ref, own_ref, chosen_ref, c_ref, both, stage,
-                 bits, codes, side_sem, first_sem, load_sem, xs, xr, zs, zr, ms, mr, ks, kr, rs, rr):
+                 bits, codes, first_sem, load_sem, xs, xr, zs, zr, ms, mr, kr, rs, rr):
     blk, far = both.at[0], both.at[1]
     half, segments, stations, width = both.shape[1], both.shape[3], both.shape[5], both.shape[6]
     scale = 1.0 / math.sqrt(segments * width)
@@ -107,7 +107,7 @@
     def load(b, mine):
         slot = keep_slot if mine else OTHER
         return pltpu.make_async_copy(
-            x_ref.at[0, 0, :, :, :, bins(b, mine)], blk.at[b, slot], load_sem.at[int(mine), b])
+            x_ref.at[0, 0, :, :, :, bins(b, mine)], blk.at[b, slot], load_sem.at[b])
 
     def load_first(q):
         return pltpu.make_async_copy(
@@ -149,7 +149,7 @@
         slot = keep_slot + e * (OTHER - keep_slot)
         return pltpu.make_async_remote_copy(
             src_ref=blk.at[b, slot, :, :, strip(q)], dst_ref=far.at[b, 2 + e, :, :, strip(q)],
-            send_sem=ks.at[parity], recv_sem=kr.at[b],
+            send_sem=ms.at[1 - parity], recv_sem=kr.at[b],
             device_id=(side_to(parity), c), device_id_type=MESH)
 
     def whole(slots, send, recv):
@@ -167,13 +167,13 @@
         return whole(c_ref.at[0, pl.ds(0, count)], rs.at[send], rr.at[code - 1])
 
     def load_codes():
-        return pltpu.make_async_copy(codes_ref, codes, side_sem.at[0])
+        return pltpu.make_async_copy(codes_ref, codes, first_sem.at[0])
 
     def load_bits():
-        return pltpu.make_async_copy(bits_ref.at[0], bits, side_sem.at[1])
+        return pltpu.make_async_copy(bits_ref.at[0], bits, first_sem.at[1])
 
     def load_old():
-        return pltpu.make_async_copy(old_ref.at[0, 0, 0], own_ref, side_sem.at[2])
+        return pltpu.make_async_copy(old_ref.at[0, 0, 0], own_ref, first_sem.at[2])
 
     def unpack():
         column = lax.broadcasted_iota(jnp.int32, (stations, stations), 0)
@@ -198,16 +198,16 @@
         return 0
 
     def send_other(b):
-        load(b, False).wait()
         whiten_rows(both, (0, b, OTHER), 0, stations)
         for q in range(PIECES):
             x_copy(b, q).start()
 
-    def send_mine(b, _):
-        load(b, True).wait()
+    def send_mine(b):
         whiten_rows(both, (0, b, keep_slot), 0, stations)
         pl.when(sends_z)(z_copy(b).start)
-        return 0
+
+    def loaded(b):
+        pltpu.make_async_copy(blk.at[b, pl.ds(0, 2)], blk.at[b, pl.ds(0, 2)], load_sem.at[b]).wait()
 
     for q in range(PIECES):
         load_first(q).start()
@@ -222,29 +222,31 @@
             def _():
                 pl.semaphore_signal(barrier, inc=1, device_id=(r + dr, col), device_id_type=MESH)
     lax.fori_loop(0, half, load_band, 0)
-    load_codes().start()
-    load_bits().start()
-    load_old().start()
     for q in range(PIECES):
         load_first(q).wait()
         whiten_rows(both, (0, 0, OTHER), q * piece, piece)
         if q == 0:
             pl.semaphore_wait(barrier, peers)
         x_copy(0, q).start()
-    lax.fori_loop(0, 2, send_mine, 0)
+    load_codes().start()
+    load_bits().start()
+    load_old().start()
+    load(0, True).wait()
+    send_mine(0)
+    loaded(1)
+    send_mine(1)
+    send_other(1)
     for step in range(AHEAD):
         for parity in (0, 1):
             pl.when(sides(parity))(side_copy(parity, jnp.int32(step)).start)
 
     def send_rest(b, _):
+        loaded(b)
         send_other(b)
-
-        @pl.when(b > 1)
-        def _():
-            send_mine(b, 0)
+        send_mine(b)
         return 0
 
-    lax.fori_loop(1, half, send_rest, 0)
+    lax.fori_loop(2, half, send_rest, 0)
 
     def own_product(b):
         for slot, band in ((keep_slot, half * odd + b), (OTHER, half * (1 - odd) + b)):
@@ -341,7 +343,7 @@
                         pl.when(below)(whole(far.at[a, 1], ms.at[0], mr.at[a, 1]).wait_recv)
                     if which == 2:
                         pl.when(meets(lax.rem(a, 2)))(
-                            whole(far.at[a, pl.ds(2, 2)], ks.at[0], kr.at[a]).wait_recv)
+                            whole(far.at[a, pl.ds(2, 2)], ms.at[0], kr.at[a]).wait_recv)
                     emit(a, table[which], (a == half - 1) & (last != which) if which in ACROSS else True)
                     if which == 7:
                         @pl.when(a == half - 1)
@@ -357,10 +359,7 @@
     whole(blk.at[:, OTHER], xs.at[0], xr.at[0, 0]).wait_send()
     pl.when(sends_z)(whole(blk.at[:, OTHER], zs.at[0], xr.at[0, 0]).wait_send)
     for d, there in ((0, below), (1, above)):
-        pl.when(there)(whole(blk.at[:, 1], ms.at[d], xr.at[0, 0]).wait_send)
-    for parity in (0, 1):
-        pl.when(sides(parity))(
-            whole(far.at[pl.ds(0, turns[parity]), pl.ds(2, 2)], ks.at[parity], xr.at[0, 0]).wait_send)
+        pl.when(there)(whole(blk.at[:, pl.ds(0, 2)], ms.at[d], xr.at[0, 0]).wait_send)
     for group, there in enumerate((right_pair, above & right_pair, below & right_pair)):
         pl.when(there)(results(half, group).wait_send)
     for group, there in enumerate((left_pair, below & left_pair, above & left_pair), 3):
@@ -396,11 +395,11 @@
             pltpu.VMEM((half, 8, 2, stations, stations), jnp.bfloat16),
             pltpu.VMEM((slots, words, 1, stations), jnp.int32),
             pltpu.SMEM(codes.shape, jnp.int32),
-            dma((3,)), dma((PIECES,)), dma((2, half)),
+            dma((PIECES,)), dma((half,)),
             dma((1,)), dma((half, PIECES)),
             dma((1,)), dma((half,)),
             dma((2,)), dma((half, 2)),
-            dma((2,)), dma((half,)),
+            dma((half,)),
             dma((7,)), dma((4,)),
         ],
         compiler_params=pltpu.CompilerParams(collective_id=0, has_side_effects=True, vmem_limit_bytes=48 * 1024 * 1024),

time: 88.6 us -> 88.5 us (level)
  no operation moved by 1% of the time
where the time goes in v5:
time: 88.5 us; the launch traced here: 86.8 us
  Pallas kernels  86.8 us (98%)
    pallas_call x1, Pallas kernels, crosses(): pl.pallas_call(functools.partial(cross_kernel, rows, cols), out_shape=(ja...  84.4 us
    pallas_call x1, Pallas kernels, combine(): pl.pallas_call(combine_kernel, out_shape=jax.ShapeDtypeStruct(old.shape,...  2.4 us

profile of v5, /device:TPU:11, one launch (start us, length us, event | category | flops | bytes accessed | tf_op | source)
XLA Modules:
  0.0 86.8 jit_solution(7706782475175786731)
XLA Ops:
  0.0 0.0 copy-start
  0.0 84.4 %crosses.1 = (f32[8,2,128,128]{3,2,1,0:T(8,128)S(1)}, f32[11,128,128]{2,1,0:T(8,128)S(1)}, bf16[4,8,2,128,128]{4,3,2,1,0:T(8,128)(2,1)S(1)}) custom-call(bf16[1,1,3,2,128,4096]{5,4,3,2,1,0:T(8,128)(2,1)} %x_ref.1, s32[5]{0:T(128)} %bitcast.3, s32[1,5,5,1,128]{4,3,2,1,0:T(1,128)} %bitcast.2, f32[1,1,5,8,2,128,128]{6,5,4,3,2,1,0:T(8,128)} %old_ref.3), custom_call_target="tpu_custom_call" | custom-call | tf_op jit(solution)/shard_map/crosses/pallas_call | solution.py:384
  84.4 0.0 copy-done
  84.4 2.4 %combine.1 = f32[1,1,5,8,2,128,128]{6,5,4,3,2,1,0:T(8,128)} custom-call(f32[8,2,128,128]{3,2,1,0:T(8,128)S(1)} %get-tuple-element.8.own_ref, f32[11,128,128]{2,1,0:T(8,128)S(1)} %get-tuple-element.9.chosen_ref, bf16[4,8,2,128,128]{4,3,2,1,0:T(8,128)(2,1)S(1)} %get-tuple-element.10.c_ref, f32[1,1,5,8,2,128,128]{6,5,4,3,2,1,0:T(8,128)S(1)} %copy-done), custom_call_target="tpu_custom_call" | custom-call | tf_op jit(solution)/shard_map/combine/pallas_call | solution.py:436
Async XLA Ops:
  0.0 84.4 %copy-start = (f32[1,1,5,8,2,128,128]{6,5,4,3,2,1,0:T(8,128)S(1)}, f32[1,1,5,8,2,128,128]{6,5,4,3,2,1,0:T(8,128)}, u32[]{:S(2)}) copy-start(f32[1,1,5,8,2,128,128]{6,5,4,3,2,1,0:T(8,128)} %old_ref.3) | copy-start | bytes 15728644

commit v6 on v5

--- a/solution.py
+++ b/solution.py
@@ -62,6 +62,7 @@
 EARLY = 1
 AHEAD = 8
 ACROSS = (1, 5, 7)
+LAST = 7
 ORDER = (1, 5, 7, 0, 4, 6, 2, 3)
 GROUP = (3, 0, 6, 6, 4, 1, 5, 2)
 
@@ -298,14 +299,14 @@
 
                 pl.when(jnp.logical_not(local))(remote)
 
-    last = jnp.where(lax.rem(r, 2) == 0, 1, jnp.where((r == 1) & (c == 1), 7, 5))
 
     def fire(a, held):
         table = routes(a)
         for which in ACROSS:
             _, _, _, code, band, row, col, present, _ = table[which]
-            turn = (last == which) == held
-            pl.when(present & turn)(r_copy(a, which, code, band, row, col).start)
+            turn = (which == LAST) == held
+            if turn:
+                pl.when(present)(r_copy(a, which, code, band, row, col).start)
 
     def step(b, _):
         for q in range(PIECES):
@@ -344,7 +345,7 @@
                     if which == 2:
                         pl.when(meets(lax.rem(a, 2)))(
                             whole(far.at[a, pl.ds(2, 2)], ms.at[0], kr.at[a]).wait_recv)
-                    emit(a, table[which], (a == half - 1) & (last != which) if which in ACROSS else True)
+                    emit(a, table[which], (a == half - 1) & (which != LAST) if which in ACROSS else True)
                     if which == 7:
                         @pl.when(a == half - 1)
                         def _():

time: 88.5 us -> 88.5 us (level)
  no operation moved by 1% of the time
where the time goes in v6:
time: 88.5 us; the launch traced here: 86.7 us
  Pallas kernels  86.7 us (98%)
    pallas_call x1, Pallas kernels, crosses(): pl.pallas_call(functools.partial(cross_kernel, rows, cols), out_shape=(ja...  84.3 us
    pallas_call x1, Pallas kernels, combine(): pl.pallas_call(combine_kernel, out_shape=jax.ShapeDtypeStruct(old.shape,...  2.4 us

profile of v6, /device:TPU:11, one launch (start us, length us, event | category | flops | bytes accessed | tf_op | source)
XLA Modules:
  0.0 86.7 jit_solution(17240275356445061036)
XLA Ops:
  0.0 0.0 copy-start
  0.0 84.3 %crosses.1 = (f32[8,2,128,128]{3,2,1,0:T(8,128)S(1)}, f32[11,128,128]{2,1,0:T(8,128)S(1)}, bf16[4,8,2,128,128]{4,3,2,1,0:T(8,128)(2,1)S(1)}) custom-call(bf16[1,1,3,2,128,4096]{5,4,3,2,1,0:T(8,128)(2,1)} %x_ref.1, s32[5]{0:T(128)} %bitcast.3, s32[1,5,5,1,128]{4,3,2,1,0:T(1,128)} %bitcast.2, f32[1,1,5,8,2,128,128]{6,5,4,3,2,1,0:T(8,128)} %old_ref.3), custom_call_target="tpu_custom_call" | custom-call | tf_op jit(solution)/shard_map/crosses/pallas_call | solution.py:385
  84.3 0.0 copy-done
  84.3 2.4 %combine.1 = f32[1,1,5,8,2,128,128]{6,5,4,3,2,1,0:T(8,128)} custom-call(f32[8,2,128,128]{3,2,1,0:T(8,128)S(1)} %get-tuple-element.8.own_ref, f32[11,128,128]{2,1,0:T(8,128)S(1)} %get-tuple-element.9.chosen_ref, bf16[4,8,2,128,128]{4,3,2,1,0:T(8,128)(2,1)S(1)} %get-tuple-element.10.c_ref, f32[1,1,5,8,2,128,128]{6,5,4,3,2,1,0:T(8,128)S(1)} %copy-done), custom_call_target="tpu_custom_call" | custom-call | tf_op jit(solution)/shard_map/combine/pallas_call | solution.py:437
Async XLA Ops:
  0.0 84.3 %copy-start = (f32[1,1,5,8,2,128,128]{6,5,4,3,2,1,0:T(8,128)S(1)}, f32[1,1,5,8,2,128,128]{6,5,4,3,2,1,0:T(8,128)}, u32[]{:S(2)}) copy-start(f32[1,1,5,8,2,128,128]{6,5,4,3,2,1,0:T(8,128)} %old_ref.3) | copy-start | bytes 15728644
